TPU v7x, 32 devices: a whole 2x2x4 slice. The times are simulated.
32 devices in a mesh: blk: 4 (over y, x), rows: 8 (over z, core).
Axes of the slice: x: 2, y: 2, z: 4, core: 2. Of those that a mesh axis runs over, the one named last changes fastest.
Arguments:
- embeddings: bfloat16 [65536, 768], P(('blk', 'rows')), may hold values from -6 to 6
- coverage: float32 [65536], P(('blk', 'rows')), may hold values from 0 to 4
- chosen_index: int32 [64], replicated, may hold values from 0 to 65535, as said below
- candidate_index: int32 [512], P('blk'), may hold values from 0 to 65535, as said below
Outputs:
- new_coverage: float32 [65536], P(('blk', 'rows'))
- gains: float32 [512], P(('blk', 'rows'))
Inputs may be any that keep to these rules, and one draw needn't show every extreme that they name: `chosen_index`: the entries are distinct; the rows r * 2048 to (r + 1) * 2048 - 1 hold at most 4 of them for every r, and exactly 4 for some r. `candidate_index`: entries b * 128 to (b + 1) * 128 - 1 lie in rows b * 16384 to (b + 1) * 16384 - 1.
All inputs are finite; a program needn't handle non-finite values.
Results may differ from a plain program's by a relative error of at most 0.00035.
Values may be sent and summed in bfloat16 or wider, within the bound.
A program may use at most 64 MiB of HBM per device.

v0:
```python
import jax
import jax.numpy as jnp
from jax import lax
from jax.sharding import PartitionSpec as P


def owned_rows(embeddings, indices, base_row):
    local_rows = embeddings.shape[0]
    offset = indices - base_row
    inside = (offset >= 0) & (offset < local_rows)
    safe = jnp.clip(offset, 0, local_rows - 1)
    picked = jnp.take(embeddings, safe, axis=0).astype(jnp.float32)
    return jnp.where(inside[:, None], picked, 0.0)


def local(embeddings, coverage, chosen_index, candidate_index):
    local_rows = embeddings.shape[0]
    width = embeddings.shape[1]
    scale = 1.0 / width**0.5
    device_pos = lax.axis_index("blk") * lax.axis_size("rows") + lax.axis_index("rows")
    base_row = device_pos * local_rows
    chosen_f = lax.psum(owned_rows(embeddings, chosen_index, base_row), ("blk", "rows"))
    chosen_rows = chosen_f.astype(jnp.bfloat16)
    sims = jnp.dot(embeddings, chosen_rows.T, preferred_element_type=jnp.float32) * scale
    best = jnp.max(sims, axis=1)
    new_coverage = jnp.maximum(coverage, best)
    block_f = lax.psum(
        owned_rows(embeddings, candidate_index, base_row).astype(jnp.bfloat16), "rows"
    )
    cand_sims = (
        jnp.dot(
            embeddings,
            lax.all_gather(block_f, "blk", axis=0, tiled=True).T,
            preferred_element_type=jnp.float32,
        )
        * scale
    )
    gain_part = jnp.sum(jnp.maximum(cand_sims - new_coverage[:, None], 0.0), axis=0)
    gains = lax.psum_scatter(gain_part, ("blk", "rows"), scatter_dimension=0, tiled=True)
    return (new_coverage, gains)


def solution(mesh):
    placed = (P(("blk", "rows"), None), P(("blk", "rows")), P(), P("blk"))
    return jax.shard_map(
        local,
        mesh=mesh,
        in_specs=placed,
        out_specs=(P(("blk", "rows")), P(("blk", "rows"))),
        check_vma=False,
    )
```

profile of v0, /device:TPU:0, one launch (start us, length us, event | category | flops | bytes accessed | tf_op | source)
XLA Modules:
  0.0 129.1 jit_solution(3781930005201907829)
XLA Ops:
  7.2 0.0 copy-start
  7.2 0.0 all-reduce.4.cloned.1.call-start
  7.2 0.8 compare_and_fusion
  8.1 1.0 copy-done
  9.1 0.0 copy-start.1
  9.1 0.9 gather_fusion.1
  9.9 0.8 select_convert_fusion
  10.8 0.0 all-reduce.4.cloned.1.call-update
  10.8 0.7 compare_and_fusion.2
  11.5 0.7 gather_fusion
  12.2 0.1 convert_select_fusion
  12.3 44.4 %all-reduce.5 = bf16[64,768]{1,0:T(8,128)(2,1)S(1)} all-reduce(f32[64,768]{1,0:T(8,128)S(1)} %convert_select_fusion), channel_id=1, replica_groups=mesh['blk'=4,'rows'=8] {'blk','rows'}, use_global_device_ids=true, to_apply=%region_0.1 | all-reduce | flops 49152 | bytes 294912 | tf_op jit(solution)/shard_map/psum | solution.py:22
  56.7 1.1 fusion
  57.8 0.0 copy-done.1
  57.8 0.0 copy-start.2
  57.8 11.1 %all-reduce.4.cloned.1.call-done = bf16[128,768]{1,0:T(8,128)(2,1)} async-done(((bf16[128,768]{1,0:T(8,128)(2,1)}), bf16[128,768]{1,0:T(8,128)(2,1)}) %all-reduce.4.cloned.1.call-update) | async-done | bytes 196624 | tf_op jit(solution)/shard_map/psum | solution.py:27
  68.9 12.4 %all_gather.3 = bf16[512,768]{1,0:T(8,128)(2,1)S(1)} all-gather(bf16[128,768]{1,0:T(8,128)(2,1)} %all-reduce.4.cloned.1.call-done), channel_id=1, replica_groups=mesh['blk'=4,'rows'=8] {'blk'}, dimensions={0}, use_global_device_ids=true | all-gather | bytes 983040 | tf_op jit(solution)/shard_map/all_gather | solution.py:33
  81.3 1.9 %maximum_reduce_fusion = f32[512]{0:T(512)S(1)} fusion(bf16[512,768]{1,0:T(8,128)(2,1)S(1)} %all_gather.3, bf16[2048,768]{1,0:T(8,128)(2,1)S(1)} %copy-done, f32[2048]{0:T(1024)S(1)} %max.18), kind=kOutput, calls=%fused_computation.2 | convolution fusion | flops 1614806528 | bytes 3942400 | tf_op jit(solution)/shard_map/dot_general | solution.py:31
  83.3 0.0 copy-done.2
  83.3 38.4 %all-reduce = f32[512]{0:T(512)S(1)} all-reduce(f32[512]{0:T(512)S(1)} %maximum_reduce_fusion), channel_id=2, replica_groups=mesh['blk'=4,'rows'=8] {'blk','rows'}, use_global_device_ids=true, to_apply=%region_4.5.clone | all-reduce | flops 512 | bytes 4096
  121.6 0.6 dynamic-slice
  (3 shorter events, 0.0 us)
Async XLA Ops:
  7.2 1.9 %copy-start = (bf16[2048,768]{1,0:T(8,128)(2,1)S(1)}, bf16[2048,768]{1,0:T(8,128)(2,1)}, u32[]{:S(2)}) copy-start(bf16[2048,768]{1,0:T(8,128)(2,1)} %param.4) | copy-start | bytes 9437188
  7.2 61.7 %all-reduce.4.cloned.1.call-start = ((), (), s32[]{:S(2)}) async-start(), calls=%async_computation | async-start | bytes 393216 | tf_op jit(solution)/shard_map/psum | solution.py:27
  9.1 48.7 %copy-start.1 = (f32[2048]{0:T(1024)S(1)}, f32[2048]{0:T(1024)}, u32[]{:S(2)}) copy-start(f32[2048]{0:T(1024)} %param.5) | copy-start | bytes 24580
  57.8 25.5 %copy-start.2 = (f32[2048]{0:T(1024)}, f32[2048]{0:T(1024)S(1)}, u32[]{:S(2)}) copy-start(f32[2048]{0:T(1024)S(1)} %max.18) | copy-start | bytes 24580
Sparse Core Ops, SparseCore 0:
  10.9 57.9 all-reduce.3
where the time goes:
time: 129 us
  blocking collectives  95.2 us (74%)
  between operations  14.1 us (11%)
  waiting for transfers between devices  11.1 us (9%)
  local copies, waits for them, and re-layouts  3.2 us (2%)
  matrix products  3 us (2%)
  other arithmetic  2.41 us (2%)
    psum x1, blocking collectives, local(): lax.psum(owned_rows(embeddings, chosen_index, base_row), ('blk', 'rows'))  44.4 us
    unnamed x1, blocking collectives  38.4 us
    all_gather x1, blocking collectives, local(): lax.all_gather(block_f, 'blk', axis=0, tiled=True)  12.4 us
    psum x1, waiting for transfers between devices, local(): lax.psum(owned_rows(embeddings, candidate_index, base_row).astype(jnp.bfl...  11.1 us
  transfers between devices with their start and end apart: 1, of which 1 were waited for; matrix products, arithmetic and copies ran while one was open for 2% of the time, Pallas kernels for 0%

commit v1 on v0

v1 whole, which is shorter than its diff:
```python
import functools

import jax
import jax.numpy as jnp
from jax import lax
from jax.experimental import pallas as pl
from jax.experimental.pallas import tpu as pltpu
from jax.sharding import PartitionSpec as P

MOST = 4
MESH = pl.DeviceIdType.MESH
NT = (((1,), (1,)), ((), ()))


def iota(shape, dim):
    return lax.broadcasted_iota(jnp.int32, shape, dim)


def log2(n):
    assert n & (n - 1) == 0
    return n.bit_length() - 1


def kernel(
    nb, nr, per, pad,
    emb_hbm, cov_ref, chosen_ref, cand_ref,
    newcov_ref, gains_ref,
    emb, mine, pair, half, part, rows_g, pack_g, ncov, gsend, grecv,
    load_sem, pair_s, pair_r, rs_s, rs_r,
    cz_s, cb_s, cs_s, c_r, kz_s, kb_s, ks_s, k_r, g_s, g_r,
):
    nz = nr // 2
    n = nb * nr
    local, width = emb.shape
    scale = 1.0 / width**0.5
    tiles = width // 128
    nk = chosen_ref.shape[1]
    nc = cand_ref.shape[1]
    length = nr * pad
    b = lax.axis_index("blk")
    r = lax.axis_index("rows")
    z = r // 2
    c = lax.rem(r, 2)
    me = b * nr + r
    base = me * local

    pieces = load_sem.shape[0]
    step = local // pieces

    def load(i):
        sl = pl.ds(i * step, step)
        return pltpu.make_async_copy(emb_hbm.at[sl], emb.at[sl], load_sem.at[i])

    for i in range(pieces):
        load(i).start()

    barrier = pltpu.get_barrier_semaphore()

    @pl.loop(1, n)
    def _(i):
        peer = lax.rem(me + i, n)
        pl.semaphore_signal(
            barrier, inc=1, device_id=(peer // nr, lax.rem(peer, nr)), device_id_type=MESH
        )

    p = iota((length, nc), 0)
    lp, lz = log2(pad), log2(nz)
    pi = p & (pad - 1)
    pz = (p >> lp) & (nz - 1)
    pc = p >> (lp + lz)
    want = ((pz * 2 + pc) * per) + pi
    pick = (want == iota((length, nc), 1)) & (pi < per)
    cand_f = (cand_ref[...] + 1).astype(jnp.float32)
    cand_col = jnp.sum(jnp.where(pick, cand_f, 0.0), axis=1, keepdims=True)
    cand_col = cand_col.astype(jnp.int32) - 1 - base

    ll = log2(local)
    ch_row = chosen_ref[...]
    sub, lane = iota((nk, nk), 0), iota((nk, nk), 1)
    ch_col = jnp.sum(
        jnp.where(sub == lane, ch_row.astype(jnp.float32), 0.0), axis=1, keepdims=True
    ).astype(jnp.int32)
    own_row, own_col = ch_row >> ll, ch_col >> ll
    same = own_row == own_col
    rank_col = jnp.sum(
        jnp.where(same & (lane < sub), 1.0, 0.0), axis=1, keepdims=True
    ).astype(jnp.int32)
    rank_row = jnp.sum(
        jnp.where(same & (sub < lane), 1.0, 0.0), axis=0, keepdims=True
    ).astype(jnp.int32)

    col = jnp.concatenate([cand_col, ch_col - base], axis=0)
    acc = jnp.zeros((length + nk, width), jnp.float32)
    for i in range(pieces):
        load(i).wait()
        hot = (col == iota((length + nk, step), 1) + i * step).astype(jnp.float32)
        acc += jnp.dot(
            hot.astype(jnp.bfloat16),
            emb[pl.ds(i * step, step), :],
            preferred_element_type=jnp.float32,
        )
    mine[...] = acc[:length].astype(jnp.bfloat16).reshape(2, nz, pad, width)
    got = acc[length:].astype(jnp.bfloat16)

    groups = 16 // MOST
    sel_sub = iota((16, nk), 0)
    for h in range(pack_g.shape[-1] // 128):
        packed = jnp.zeros((16, 128), jnp.float32)
        for t in range(h * groups, min(tiles, (h + 1) * groups)):
            sel = (own_row == me) & (sel_sub == (t % groups) * MOST + rank_row)
            packed += jnp.dot(
                sel.astype(jnp.float32).astype(jnp.bfloat16),
                got[:, t * 128 : (t + 1) * 128],
                preferred_element_type=jnp.float32,
            )
        pack_g[b, c, z, :, h * 128 : (h + 1) * 128] = packed.astype(jnp.bfloat16)

    pl.semaphore_wait(barrier, n - 1)

    def remote(src, dst, ss, rs, pb, pz_, pc_):
        return pltpu.make_async_remote_copy(
            src_ref=src, dst_ref=dst, send_sem=ss, recv_sem=rs,
            device_id=(pb, pz_ * 2 + pc_), device_id_type=MESH,
        )

    def other(i, count, k):
        return lax.rem(i + k, count)

    class Gather:
        def __init__(self, buf, zs, bs, ss, rs):
            self.buf, self.zs, self.bs, self.ss, self.rs = buf, zs, bs, ss, rs

        def to_z(self, k):
            at = self.buf.at[b, c, z]
            return remote(at, at, self.zs.at[k], self.rs.at[b, c, z], b, other(z, nz, k), c)

        def to_b(self, zz, k):
            at = self.buf.at[b, c, zz]
            return remote(
                at, at, self.bs.at[zz, k], self.rs.at[b, c, zz], other(b, nb, k), z, c
            )

        def to_s(self, bb, zz):
            at = self.buf.at[bb, c, zz]
            return remote(at, at, self.ss.at[bb, zz], self.rs.at[bb, c, zz], b, z, 1 - c)

        def wait(self, bb, cc, zz):
            at = self.buf.at[bb, cc, zz]
            remote(at, at, self.zs.at[0], self.rs.at[bb, cc, zz], b, z, 1 - c).wait_recv()

        def start(self):
            for k in range(1, nz):
                self.to_z(k).start()
            self.spread(z)

        def spread(self, zz):
            for k in range(1, nb):
                self.to_b(zz, k).start()
            self.to_s(b, zz).start()

        def column(self):
            for k in range(1, nz):
                zz = other(z, nz, k)
                self.wait(b, c, zz)
                self.spread(zz)

        def blocks(self, k):
            bb = other(b, nb, k)
            for j in range(nz):
                zz = other(z, nz, j)
                self.wait(bb, c, zz)
                self.to_s(bb, zz).start()

        def sibling(self, bb):
            for zz in range(nz):
                self.wait(bb, 1 - c, zz)

        def drain(self):
            for k in range(1, nz):
                self.to_z(k).wait_send()
            for zz in range(nz):
                for k in range(1, nb):
                    self.to_b(zz, k).wait_send()
                for bb in range(nb):
                    self.to_s(bb, zz).wait_send()

    chosen = Gather(pack_g, cz_s, cb_s, cs_s, c_r)
    cands = Gather(rows_g, kz_s, kb_s, ks_s, k_r)

    swap = remote(mine.at[1 - c], pair, pair_s, pair_r, b, z, 1 - c)
    swap.start()
    chosen.start()
    swap.wait_recv()
    half[...] = mine[c] + pair[...]

    def scatter(k):
        to = other(z, nz, k)
        return remote(half.at[to], part.at[z], rs_s.at[k], rs_r.at[z], b, to, c)

    for k in range(1, nz):
        scatter(k).start()
    chosen.column()
    total = half[z]
    for k in range(1, nz):
        zz = other(z, nz, k)
        remote(half.at[zz], part.at[zz], rs_s.at[k], rs_r.at[zz], b, zz, c).wait_recv()
        total = total + part[zz]
    rows_g[b, c, z] = total
    cands.start()
    for k in range(1, nb):
        chosen.blocks(k)
    cands.column()
    for k in range(nb):
        chosen.sibling(other(b, nb, k))

    packs = pack_g[...].reshape(n * 16, pack_g.shape[-1])
    spot_r = own_col - ((own_col >> log2(nr)) << log2(nr))
    spot_b = own_col >> log2(nr)
    spot = ((spot_b * 2 + (spot_r & 1)) * nz + (spot_r >> 1)) * 16 + rank_col
    place = iota((nk, n * 16), 1)
    best = None
    for t in range(tiles):
        pull = (place == spot + (t % groups) * MOST).astype(jnp.float32)
        h = t // groups
        rows_t = jnp.dot(
            pull.astype(jnp.bfloat16),
            packs[:, h * 128 : (h + 1) * 128],
            preferred_element_type=jnp.float32,
        ).astype(jnp.bfloat16)
        best = rows_t if best is None else jnp.concatenate([best, rows_t], axis=1)
    span = 512
    for i in range(local // span):
        sl = pl.ds(i * span, span)
        s = lax.dot_general(best, emb[sl, :], NT, preferred_element_type=jnp.float32)
        top = jnp.max(s * scale, axis=0, keepdims=True)
        new = jnp.maximum(cov_ref[:, sl], top)
        ncov[:, sl] = new
        newcov_ref[:, sl] = new

    def send_gain(bb, rr):
        to = bb * nr + rr
        return pltpu.make_async_remote_copy(
            src_ref=gsend.at[bb], dst_ref=grecv.at[me],
            send_sem=g_s.at[to], recv_sem=g_r.at[me],
            device_id=(bb, rr), device_id_type=MESH,
        )

    def block_gain(bb):
        g = rows_g[bb].reshape(length, width)
        fold = jnp.zeros((length, 128), jnp.float32)
        for i in range(local // span):
            sl = pl.ds(i * span, span)
            s = lax.dot_general(g, emb[sl, :], NT, preferred_element_type=jnp.float32)
            x = jnp.maximum(s * scale - ncov[:, sl], 0.0)
            for j in range(span // 128):
                fold += x[:, j * 128 : (j + 1) * 128]
        return jnp.sum(fold.T, axis=0, keepdims=True)

    cands.sibling(b)
    gain = block_gain(b)
    gsend[b] = gain
    grecv[me] = gain
    for k in range(1, nr):
        send_gain(b, other(r, nr, k)).start()
    for k in range(1, nb):
        cands.blocks(k)
    for k in range(1, nb):
        bb = other(b, nb, k)
        cands.sibling(bb)
        gsend[bb] = block_gain(bb)
        for j in range(nr):
            send_gain(bb, other(r, nr, j)).start()

    swap.wait_send()
    for k in range(1, nz):
        scatter(k).wait_send()
    chosen.drain()
    cands.drain()

    @pl.loop(1, n)
    def _(i):
        src = lax.rem(me + i, n)
        pltpu.make_async_remote_copy(
            src_ref=gsend.at[b], dst_ref=grecv.at[src],
            send_sem=g_s.at[src], recv_sem=g_r.at[src],
            device_id=(src // nr, lax.rem(src, nr)), device_id_type=MESH,
        ).wait()

    total_g = jnp.sum(grecv[...].reshape(n, length), axis=0, keepdims=True)
    wide = jnp.broadcast_to(total_g, (8, length))
    at = (c * nz + z) * pad
    wide = pltpu.roll(wide, lax.rem(length - at, length), 1)
    gains_ref[...] = wide[0:1, :per]


def local_fn(nb, nr, embeddings, coverage, chosen_index, candidate_index):
    local, width = embeddings.shape
    nc = candidate_index.shape[0]
    nk = chosen_index.shape[0]
    per = nc // nr
    pad = max(per, 16)
    nz = nr // 2
    n = nb * nr
    length = nr * pad
    lanes = 128 * pl.cdiv(width // 128, 16 // MOST)
    bf, f32 = jnp.bfloat16, jnp.float32
    dma = pltpu.SemaphoreType.DMA
    vmem = pl.BlockSpec(memory_space=pltpu.VMEM)
    gather_sems = [dma((nz,)), dma((nz, nb)), dma((nb, nz)), dma((nb, 2, nz))]
    new, gains = pl.pallas_call(
        functools.partial(kernel, nb, nr, per, pad),
        out_shape=(
            jax.ShapeDtypeStruct((1, local), f32),
            jax.ShapeDtypeStruct((1, per), f32),
        ),
        in_specs=[pl.BlockSpec(memory_space=pl.ANY), vmem, vmem, vmem],
        out_specs=(vmem, vmem),
        scratch_shapes=[
            pltpu.VMEM((local, width), bf),
            pltpu.VMEM((2, nz, pad, width), bf),
            pltpu.VMEM((nz, pad, width), bf),
            pltpu.VMEM((nz, pad, width), bf),
            pltpu.VMEM((nz, pad, width), bf),
            pltpu.VMEM((nb, 2, nz, pad, width), bf),
            pltpu.VMEM((nb, 2, nz, 16, lanes), bf),
            pltpu.VMEM((1, local), f32),
            pltpu.VMEM((nb, 1, length), f32),
            pltpu.VMEM((n, 1, length), f32),
            dma((4,)), dma, dma, dma((nz,)), dma((nz,)),
            *gather_sems, *gather_sems, dma((n,)), dma((n,)),
        ],
        compiler_params=pltpu.CompilerParams(
            collective_id=0, has_side_effects=True, vmem_limit_bytes=60 * 2**20
        ),
    )(
        embeddings,
        coverage.reshape(1, local),
        chosen_index.reshape(1, nk),
        candidate_index.reshape(1, nc),
    )
    return new.reshape(local), gains.reshape(per)


def solution(mesh):
    nb, nr = mesh.shape["blk"], mesh.shape["rows"]
    placed = (P(("blk", "rows"), None), P(("blk", "rows")), P(), P("blk"))
    return jax.shard_map(
        functools.partial(local_fn, nb, nr),
        mesh=mesh,
        in_specs=placed,
        out_specs=(P(("blk", "rows")), P(("blk", "rows"))),
        check_vma=False,
    )
```

time: 129 us -> 35.2 us (0.27)
  blocking collectives: 95.2 us -> 0 us
  Pallas kernels: 0 us -> 31.9 us
  between operations: 14.1 us -> 0.64 us
  waiting for transfers between devices: 11.1 us -> 0 us
  matrix products: 3 us -> 0 us
  other arithmetic: 2.41 us -> 0 us
    psum x1 -> x0, blocking collectives: 44.4 us -> none  [local(): lax.psum(owned_rows(embeddings, chosen_index, base_row), ('blk', 'rows'))]
    unnamed x1 -> x0, blocking collectives: 38.4 us -> none
    pallas_call x0 -> x1, Pallas kernels: none -> 31.9 us  [local_fn(): pl.pallas_call(functools.partial(kernel, nb, nr, per, pad), out_shape=(ja...]
    all_gather x1 -> x0, blocking collectives: 12.4 us -> none  [local(): lax.all_gather(block_f, 'blk', axis=0, tiled=True)]
    psum x1 -> x0, waiting for transfers between devices: 11.1 us -> none  [local(): lax.psum(owned_rows(embeddings, candidate_index, base_row).astype(jnp.bfl...]
    dot_general x2 -> x0, matrix products: 3 us -> none  [the longest x1 1.92 us: local(): jnp.dot(embeddings, lax.all_gather(block_f, 'blk', axis=0, tiled=True).T,...]
    gather x2 -> x0, local copies, waits for them, and re-layouts: 1.58 us -> none  [owned_rows(): picked = jnp.take(embeddings, safe, axis=0).astype(jnp.float32)]
    and x2 -> x0, other arithmetic: 1.49 us -> none  [owned_rows(): picked = jnp.take(embeddings, safe, axis=0).astype(jnp.float32)]
  transfers between devices with their start and end apart: 1 -> 0, of which waited for: 1 -> 0; matrix products, arithmetic and copies ran while one was open for 2% -> 0% of each run, Pallas kernels for 0% -> 0%
where the time goes in v1:
time: 35.2 us; the launch traced here: 35 us
  Pallas kernels  31.9 us (91%)
  local copies, waits for them, and re-layouts  2.43 us (7%)
  between operations  0.64 us (2%)
    pallas_call x1, Pallas kernels, local_fn(): pl.pallas_call(functools.partial(kernel, nb, nr, per, pad), out_shape=(ja...  31.9 us
    unnamed x2, local copies, waits for them, and re-layouts  2.43 us

profile of v1, /device:TPU:0, one launch (start us, length us, event | category | flops | bytes accessed | tf_op | source)
XLA Modules:
  0.0 35.0 jit_solution(9676562362281337297)
XLA Ops:
  0.6 31.9 %shard_map.59 = (f32[1,2048]{1,0:T(1,128)}, f32[1,16]{1,0:T(1,128)}) custom-call(bf16[2048,768]{1,0:T(8,128)(2,1)} %emb_hbm.1, f32[1,2048]{1,0:T(1,128)} %bitcast.5, s32[1,64]{1,0:T(1,128)} %bitcast.7, s32[1,128]{1,0:T(1,128)} %bitcast.8), custom_call_target="tpu_custom_call" | custom-call | tf_op jit(solution)/shard_map/pallas_call | solution.py:310
  32.5 1.3 %copy.8 = f32[2048]{0:T(1024)} copy(f32[2048]{0:T(1024)} %bitcast.6) | data formatting | bytes 16384
  33.8 1.1 %copy.9 = f32[16]{0:T(128)} copy(f32[16]{0:T(128)} %bitcast.9) | data formatting | bytes 128

commit v2 on v1

--- a/solution.py
+++ b/solution.py
@@ -37,6 +37,7 @@
     nk = chosen_ref.shape[1]
     nc = cand_ref.shape[1]
     length = nr * pad
+    group = nb * 2 * pad
     b = lax.axis_index("blk")
     r = lax.axis_index("rows")
     z = r // 2
@@ -113,7 +114,7 @@
                 got[:, t * 128 : (t + 1) * 128],
                 preferred_element_type=jnp.float32,
             )
-        pack_g[b, c, z, :, h * 128 : (h + 1) * 128] = packed.astype(jnp.bfloat16)
+        pack_g[z, b, c, :, h * 128 : (h + 1) * 128] = packed.astype(jnp.bfloat16)
 
     pl.semaphore_wait(barrier, n - 1)
 
@@ -124,28 +125,32 @@
         )
 
     def other(i, count, k):
-        return lax.rem(i + k, count)
+        out = i
+        for bit in range(log2(count)):
+            if (k >> bit) & 1:
+                out = out + (1 - 2 * lax.rem(i // 2**bit, 2)) * 2**bit
+        return out
 
     class Gather:
         def __init__(self, buf, zs, bs, ss, rs):
             self.buf, self.zs, self.bs, self.ss, self.rs = buf, zs, bs, ss, rs
 
         def to_z(self, k):
-            at = self.buf.at[b, c, z]
+            at = self.buf.at[z, b, c]
             return remote(at, at, self.zs.at[k], self.rs.at[b, c, z], b, other(z, nz, k), c)
 
         def to_b(self, zz, k):
-            at = self.buf.at[b, c, zz]
+            at = self.buf.at[zz, b, c]
             return remote(
                 at, at, self.bs.at[zz, k], self.rs.at[b, c, zz], other(b, nb, k), z, c
             )
 
         def to_s(self, bb, zz):
-            at = self.buf.at[bb, c, zz]
+            at = self.buf.at[zz, bb, c]
             return remote(at, at, self.ss.at[bb, zz], self.rs.at[bb, c, zz], b, z, 1 - c)
 
         def wait(self, bb, cc, zz):
-            at = self.buf.at[bb, cc, zz]
+            at = self.buf.at[zz, bb, cc]
             remote(at, at, self.zs.at[0], self.rs.at[bb, cc, zz], b, z, 1 - c).wait_recv()
 
         def start(self):
@@ -158,21 +163,19 @@
                 self.to_b(zz, k).start()
             self.to_s(b, zz).start()
 
-        def column(self):
-            for k in range(1, nz):
-                zz = other(z, nz, k)
-                self.wait(b, c, zz)
-                self.spread(zz)
-
-        def blocks(self, k):
-            bb = other(b, nb, k)
-            for j in range(nz):
-                zz = other(z, nz, j)
+        def hop(self, k):
+            zz = other(z, nz, k)
+            self.wait(b, c, zz)
+            self.spread(zz)
+
+        def across(self, zz):
+            for k in range(1, nb):
+                bb = other(b, nb, k)
                 self.wait(bb, c, zz)
                 self.to_s(bb, zz).start()
 
-        def sibling(self, bb):
-            for zz in range(nz):
+        def sibling(self, zz):
+            for bb in range(nb):
                 self.wait(bb, 1 - c, zz)
 
         def drain(self):
@@ -199,24 +202,25 @@
 
     for k in range(1, nz):
         scatter(k).start()
-    chosen.column()
+    for k in range(1, nz):
+        chosen.hop(k)
     total = half[z]
     for k in range(1, nz):
         zz = other(z, nz, k)
         remote(half.at[zz], part.at[zz], rs_s.at[k], rs_r.at[zz], b, zz, c).wait_recv()
         total = total + part[zz]
-    rows_g[b, c, z] = total
+    rows_g[z, b, c] = total
     cands.start()
-    for k in range(1, nb):
-        chosen.blocks(k)
-    cands.column()
-    for k in range(nb):
-        chosen.sibling(other(b, nb, k))
+    for k in range(nz):
+        chosen.across(other(z, nz, k))
+    cands.hop(1)
+    for k in range(nz):
+        chosen.sibling(other(z, nz, k))
 
     packs = pack_g[...].reshape(n * 16, pack_g.shape[-1])
     spot_r = own_col - ((own_col >> log2(nr)) << log2(nr))
     spot_b = own_col >> log2(nr)
-    spot = ((spot_b * 2 + (spot_r & 1)) * nz + (spot_r >> 1)) * 16 + rank_col
+    spot = (((spot_r >> 1) * nb + spot_b) * 2 + (spot_r & 1)) * 16 + rank_col
     place = iota((nk, n * 16), 1)
     best = None
     for t in range(tiles):
@@ -237,17 +241,18 @@
         ncov[:, sl] = new
         newcov_ref[:, sl] = new
 
-    def send_gain(bb, rr):
+    def send_gain(zz, bb, cc):
+        rr = zz * 2 + cc
         to = bb * nr + rr
         return pltpu.make_async_remote_copy(
-            src_ref=gsend.at[bb], dst_ref=grecv.at[me],
+            src_ref=gsend.at[zz], dst_ref=grecv.at[me],
             send_sem=g_s.at[to], recv_sem=g_r.at[me],
             device_id=(bb, rr), device_id_type=MESH,
         )
 
-    def block_gain(bb):
-        g = rows_g[bb].reshape(length, width)
-        fold = jnp.zeros((length, 128), jnp.float32)
+    def group_gain(zz):
+        g = rows_g[zz].reshape(group, width)
+        fold = jnp.zeros((group, 128), jnp.float32)
         for i in range(local // span):
             sl = pl.ds(i * span, span)
             s = lax.dot_general(g, emb[sl, :], NT, preferred_element_type=jnp.float32)
@@ -256,20 +261,23 @@
                 fold += x[:, j * 128 : (j + 1) * 128]
         return jnp.sum(fold.T, axis=0, keepdims=True)
 
-    cands.sibling(b)
-    gain = block_gain(b)
-    gsend[b] = gain
-    grecv[me] = gain
-    for k in range(1, nr):
-        send_gain(b, other(r, nr, k)).start()
-    for k in range(1, nb):
-        cands.blocks(k)
-    for k in range(1, nb):
-        bb = other(b, nb, k)
-        cands.sibling(bb)
-        gsend[bb] = block_gain(bb)
-        for j in range(nr):
-            send_gain(bb, other(r, nr, j)).start()
+    for k in range(2, nz):
+        cands.hop(k)
+    cands.across(z)
+    for j in range(nz):
+        zz = other(z, nz, j)
+        if j + 1 < nz:
+            cands.across(other(z, nz, j + 1))
+        cands.sibling(zz)
+        gain = group_gain(zz)
+        gsend[zz] = gain
+        if j == 0:
+            grecv[me] = gain
+        for k in range(nb):
+            bb = other(b, nb, k)
+            if j or k:
+                send_gain(zz, bb, c).start()
+            send_gain(zz, bb, 1 - c).start()
 
     swap.wait_send()
     for k in range(1, nz):
@@ -281,15 +289,15 @@
     def _(i):
         src = lax.rem(me + i, n)
         pltpu.make_async_remote_copy(
-            src_ref=gsend.at[b], dst_ref=grecv.at[src],
+            src_ref=gsend.at[z], dst_ref=grecv.at[src],
             send_sem=g_s.at[src], recv_sem=g_r.at[src],
             device_id=(src // nr, lax.rem(src, nr)), device_id_type=MESH,
         ).wait()
 
-    total_g = jnp.sum(grecv[...].reshape(n, length), axis=0, keepdims=True)
-    wide = jnp.broadcast_to(total_g, (8, length))
-    at = (c * nz + z) * pad
-    wide = pltpu.roll(wide, lax.rem(length - at, length), 1)
+    total_g = jnp.sum(grecv[...].reshape(n, group), axis=0, keepdims=True)
+    wide = jnp.broadcast_to(total_g, (8, group))
+    at = (b * 2 + c) * pad
+    wide = pltpu.roll(wide, lax.rem(group - at, group), 1)
     gains_ref[...] = wide[0:1, :per]
 
 
@@ -301,7 +309,7 @@
     pad = max(per, 16)
     nz = nr // 2
     n = nb * nr
-    length = nr * pad
+    group = nb * 2 * pad
     lanes = 128 * pl.cdiv(width // 128, 16 // MOST)
     bf, f32 = jnp.bfloat16, jnp.float32
     dma = pltpu.SemaphoreType.DMA
@@ -321,11 +329,11 @@
             pltpu.VMEM((nz, pad, width), bf),
             pltpu.VMEM((nz, pad, width), bf),
             pltpu.VMEM((nz, pad, width), bf),
-            pltpu.VMEM((nb, 2, nz, pad, width), bf),
-            pltpu.VMEM((nb, 2, nz, 16, lanes), bf),
+            pltpu.VMEM((nz, nb, 2, pad, width), bf),
+            pltpu.VMEM((nz, nb, 2, 16, lanes), bf),
             pltpu.VMEM((1, local), f32),
-            pltpu.VMEM((nb, 1, length), f32),
-            pltpu.VMEM((n, 1, length), f32),
+            pltpu.VMEM((nz, 1, group), f32),
+            pltpu.VMEM((n, 1, group), f32),
             dma((4,)), dma, dma, dma((nz,)), dma((nz,)),
             *gather_sems, *gather_sems, dma((n,)), dma((n,)),
         ],

time: 35.2 us -> 35.3 us (level)
  no operation moved by 1% of the time
where the time goes in v2:
time: 35.3 us; the launch traced here: 35.1 us
  Pallas kernels  32 us (91%)
  local copies, waits for them, and re-layouts  2.43 us (7%)
  between operations  0.64 us (2%)
    pallas_call x1, Pallas kernels, local_fn(): pl.pallas_call(functools.partial(kernel, nb, nr, per, pad), out_shape=(ja...  32 us
    unnamed x2, local copies, waits for them, and re-layouts  2.43 us

profile of v2, /device:TPU:0, one launch (start us, length us, event | category | flops | bytes accessed | tf_op | source)
XLA Modules:
  0.0 35.1 jit_solution(13536021944733833193)
XLA Ops:
  0.6 32.0 %shard_map.59 = (f32[1,2048]{1,0:T(1,128)}, f32[1,16]{1,0:T(1,128)}) custom-call(bf16[2048,768]{1,0:T(8,128)(2,1)} %emb_hbm.1, f32[1,2048]{1,0:T(1,128)} %bitcast.5, s32[1,64]{1,0:T(1,128)} %bitcast.7, s32[1,128]{1,0:T(1,128)} %bitcast.8), custom_call_target="tpu_custom_call" | custom-call | tf_op jit(solution)/shard_map/pallas_call | solution.py:318
  32.7 1.3 %copy.8 = f32[2048]{0:T(1024)} copy(f32[2048]{0:T(1024)} %bitcast.6) | data formatting | bytes 16384
  34.0 1.1 %copy.9 = f32[16]{0:T(128)} copy(f32[16]{0:T(128)} %bitcast.9) | data formatting | bytes 128

commit v3 on v2

--- a/solution.py
+++ b/solution.py
@@ -238,8 +238,10 @@
         s = lax.dot_general(best, emb[sl, :], NT, preferred_element_type=jnp.float32)
         top = jnp.max(s * scale, axis=0, keepdims=True)
         new = jnp.maximum(cov_ref[:, sl], top)
-        ncov[:, sl] = new
         newcov_ref[:, sl] = new
+        for j in range(span // 128):
+            row = new[:, j * 128 : (j + 1) * 128]
+            ncov[pl.ds(i * span + j * 128, 128), :] = jnp.broadcast_to(row, (128, 128)).T
 
     def send_gain(zz, bb, cc):
         rr = zz * 2 + cc
@@ -252,14 +254,14 @@
 
     def group_gain(zz):
         g = rows_g[zz].reshape(group, width)
-        fold = jnp.zeros((group, 128), jnp.float32)
+        fold = [jnp.zeros((1, 128), jnp.float32)] * (group // 128)
         for i in range(local // span):
             sl = pl.ds(i * span, span)
-            s = lax.dot_general(g, emb[sl, :], NT, preferred_element_type=jnp.float32)
-            x = jnp.maximum(s * scale - ncov[:, sl], 0.0)
-            for j in range(span // 128):
-                fold += x[:, j * 128 : (j + 1) * 128]
-        return jnp.sum(fold.T, axis=0, keepdims=True)
+            s = lax.dot_general(emb[sl, :], g, NT, preferred_element_type=jnp.float32)
+            for j in range(group // 128):
+                x = jnp.maximum(s[:, j * 128 : (j + 1) * 128] * scale - ncov[sl, :], 0.0)
+                fold[j] = fold[j] + jnp.sum(x, axis=0, keepdims=True)
+        return fold[0] if len(fold) == 1 else jnp.concatenate(fold, axis=1)
 
     for k in range(2, nz):
         cands.hop(k)
@@ -331,7 +333,7 @@
             pltpu.VMEM((nz, pad, width), bf),
             pltpu.VMEM((nz, nb, 2, pad, width), bf),
             pltpu.VMEM((nz, nb, 2, 16, lanes), bf),
-            pltpu.VMEM((1, local), f32),
+            pltpu.VMEM((local, 128), f32),
             pltpu.VMEM((nz, 1, group), f32),
             pltpu.VMEM((n, 1, group), f32),
             dma((4,)), dma, dma, dma((nz,)), dma((nz,)),

time: 35.3 us -> 34.5 us (0.977)
  Pallas kernels: 32 us -> 31.2 us
    pallas_call x1, Pallas kernels: 32 us -> 31.2 us  [local_fn(): pl.pallas_call(functools.partial(kernel, nb, nr, per, pad), out_shape=(ja...]
where the time goes in v3:
time: 34.5 us; the launch traced here: 34.3 us
  Pallas kernels  31.2 us (90%)
  local copies, waits for them, and re-layouts  2.43 us (7%)
  between operations  0.64 us (2%)
    pallas_call x1, Pallas kernels, local_fn(): pl.pallas_call(functools.partial(kernel, nb, nr, per, pad), out_shape=(ja...  31.2 us
    unnamed x2, local copies, waits for them, and re-layouts  2.43 us

profile of v3, /device:TPU:0, one launch (start us, length us, event | category | flops | bytes accessed | tf_op | source)
XLA Modules:
  0.0 34.3 jit_solution(783046433939528780)
XLA Ops:
  0.6 31.2 %shard_map.59 = (f32[1,2048]{1,0:T(1,128)}, f32[1,16]{1,0:T(1,128)}) custom-call(bf16[2048,768]{1,0:T(8,128)(2,1)} %emb_hbm.1, f32[1,2048]{1,0:T(1,128)} %bitcast.5, s32[1,64]{1,0:T(1,128)} %bitcast.7, s32[1,128]{1,0:T(1,128)} %bitcast.8), custom_call_target="tpu_custom_call" | custom-call | tf_op jit(solution)/shard_map/pallas_call | solution.py:320
  31.8 1.3 %copy.8 = f32[2048]{0:T(1024)} copy(f32[2048]{0:T(1024)} %bitcast.6) | data formatting | bytes 16384
  33.1 1.1 %copy.9 = f32[16]{0:T(128)} copy(f32[16]{0:T(128)} %bitcast.9) | data formatting | bytes 128
